TPU v7x, 32 devices: a whole 2x2x4 slice. The times are simulated.
32 devices in a mesh: groups: 2 (over x), seq: 16 (over z, y, core).
Axes of the slice: x: 2, y: 2, z: 4, core: 2. Of those that a mesh axis runs over, the one named last changes fastest.
Arguments:
- queries: bfloat16 [4096, 1792], P(('groups', 'seq')), parts along dimension 0, may hold values from -100 to 100
- key_rows: bfloat16 [4096, 256], P(('groups', 'seq')), parts along dimension 0, may hold values from -100 to 100
- value_rows: bfloat16 [4096, 256], P(('groups', 'seq')), parts along dimension 0, may hold values from -6 to 6
- span_order: int32 [64], P('groups'), parts along dimension 0, may hold values from 0 to 31, each once
- kept_blocks: int32 [4, 1], P('groups'), parts along dimension 0, may hold values from 0 to 3, as said below
Outputs:
- attended: bfloat16 [4096, 1792], P(('groups', 'seq')), parts along dimension 0
- kept_cache: bfloat16 [1024, 512], P(('groups', 'seq')), parts along dimension 0
There are 2 independent parts, one for each index of `groups`. A program takes and returns all parts, laid end to end along the dimension named above; each array names one. Nothing has to cross between parts.
Inputs may be any that keep to these rules, and one draw needn't show every extreme that they name: `kept_blocks`: each row lists 1 different blocks.
All inputs are finite; a program needn't handle non-finite values.
Results may differ from a plain program's by a relative error of at most 0.0055.
Values may be sent and summed in bfloat16 or wider, within the bound.
A program may use at most 64 MiB of HBM per device.

v0:
```python
import math
import jax
import jax.numpy as jnp
from jax import lax
from jax.sharding import PartitionSpec as P

HEAD_DIM = 128
BLOCK = 512


def token_positions(span_order, span_len):
    within = jnp.arange(span_len, dtype=jnp.int32)
    return (span_order[:, None] * span_len + within[None, :]).reshape(-1)


def cache_sources(kept_blocks, row_ids):
    block_ids = row_ids // BLOCK
    match = (
        jnp.arange(kept_blocks.shape[1], dtype=jnp.int32)[None, None, :] == block_ids[None, :, None]
    )
    chosen = jnp.sum(jnp.where(match, kept_blocks[:, None, :], 0), axis=-1)
    return chosen * BLOCK + row_ids[None, :] % BLOCK


def local(queries, key_rows, value_rows, span_order, kept_blocks):
    seq_count = lax.axis_size("seq")
    my_index = lax.axis_index("seq")
    query_rows = queries.shape[0]
    kv_heads = key_rows.shape[1] // HEAD_DIM
    group_size = queries.shape[1] // key_rows.shape[1]
    scale = 1.0 / math.sqrt(HEAD_DIM)
    positions = token_positions(span_order, query_rows // 2)
    query_pos = lax.dynamic_slice_in_dim(positions, my_index * query_rows, query_rows)
    query_heads = queries.reshape(query_rows, kv_heads, group_size, HEAD_DIM)
    cache_local = kept_blocks.shape[1] * BLOCK // seq_count
    cache_src = cache_sources(
        kept_blocks, my_index * cache_local + jnp.arange(cache_local, dtype=jnp.int32)
    )

    def pick_rows(sources, key_part, value_part, part_pos):
        onehot = (sources[:, :, None] == part_pos[None, None, :]).astype(jnp.bfloat16)
        count = key_part.shape[0]
        out_rows = sources.shape[1]
        picked_keys = jnp.einsum(
            "hrk,khd->rhd",
            onehot,
            key_part.reshape(count, kv_heads, HEAD_DIM),
            preferred_element_type=jnp.float32,
        )
        picked_values = jnp.einsum(
            "hrk,khd->rhd",
            onehot,
            value_part.reshape(count, kv_heads, HEAD_DIM),
            preferred_element_type=jnp.float32,
        )
        return jnp.concatenate(
            [picked_keys.reshape(out_rows, -1), picked_values.reshape(out_rows, -1)], axis=1
        )

    def attend_block(state, block_keys, block_values, block_pos):
        running_max, totals, accum = (state[0], state[1], state[2])
        count = block_keys.shape[0]
        scores = (
            jnp.einsum(
                "qhgd,khd->hgqk",
                query_heads,
                block_keys.reshape(count, kv_heads, HEAD_DIM),
                preferred_element_type=jnp.float32,
            )
            * scale
        )
        visible = block_pos[None, None, None, :] <= query_pos[None, None, :, None]
        scores = jnp.where(visible, scores, -1e30)
        new_max = jnp.maximum(running_max, jnp.max(scores, axis=-1))
        weights = jnp.where(visible, jnp.exp(scores - new_max[..., None]), 0.0)
        factor = jnp.exp(running_max - new_max)
        totals = totals * factor + jnp.sum(weights, axis=-1)
        mixed = jnp.einsum(
            "hgqk,khd->hgqd",
            weights.astype(jnp.bfloat16),
            block_values.reshape(count, kv_heads, HEAD_DIM),
            preferred_element_type=jnp.float32,
        )
        accum = accum * factor[..., None] + mixed
        return (new_max, totals, accum)

    initial = (
        jnp.full((kv_heads, group_size, query_rows), -1e30, jnp.float32),
        jnp.zeros((kv_heads, group_size, query_rows), jnp.float32),
        jnp.zeros((kv_heads, group_size, query_rows, HEAD_DIM), jnp.float32),
    )
    initial = initial + (jnp.zeros((cache_local, 2 * kv_heads * HEAD_DIM), jnp.float32),)
    piece_keys = lax.all_gather(key_rows, "seq", axis=0, tiled=True)
    piece_values = lax.all_gather(value_rows, "seq", axis=0, tiled=True)
    count = piece_keys.shape[0]
    width = math.gcd(count, 512)

    def inner(step_index, inner_state):
        offset = (step_index * width).astype(jnp.int32)
        block_keys = lax.dynamic_slice_in_dim(piece_keys, offset, width, 0)
        block_values = lax.dynamic_slice_in_dim(piece_values, offset, width, 0)
        block_pos = lax.dynamic_slice_in_dim(positions, offset, width)
        updated = attend_block(inner_state, block_keys, block_values, block_pos)
        extra = (inner_state[3] + pick_rows(cache_src, block_keys, block_values, block_pos),)
        return updated + extra

    final = lax.fori_loop(0, count // width, inner, initial)
    attended = final[2] / final[1][..., None]
    attended = jnp.transpose(attended, (2, 0, 1, 3)).reshape(query_rows, -1).astype(jnp.bfloat16)
    kept_cache = final[3].astype(jnp.bfloat16)
    return (attended, kept_cache)


def solution(mesh):
    placed = (
        P(("groups", "seq"), None),
        P(("groups", "seq"), None),
        P(("groups", "seq"), None),
        P("groups"),
        P("groups", None),
    )
    return jax.shard_map(
        local,
        mesh=mesh,
        in_specs=placed,
        out_specs=(P(("groups", "seq"), None), P(("groups", "seq"), None)),
        check_vma=False,
    )
```

profile of v0, /device:TPU:0, one launch (start us, length us, event | category | flops | bytes accessed | tf_op | source)
XLA Modules:
  0.0 120.7 jit_solution(2158012903326060525)
XLA Ops:
  7.2 1.6 %copy.16 = bf16[128,256]{0,1:T(8,128)(2,1)} copy(bf16[128,256]{1,0:T(8,128)(2,1)} %param.8) | data formatting | bytes 131072 | tf_op args[1]
  8.9 1.6 %copy.18 = bf16[128,256]{0,1:T(8,128)(2,1)} copy(bf16[128,256]{1,0:T(8,128)(2,1)} %param.9) | data formatting | bytes 131072 | tf_op args[2]
  10.5 0.7 broadcast_multiply_fusion
  11.3 1.3 %copy.17 = bf16[128,1792]{0,1:T(8,128)(2,1)S(1)} copy(bf16[128,1792]{1,0:T(8,128)(2,1)} %param.7) | data formatting | bytes 917504 | tf_op args[0]
  12.6 0.3 copy.19
  12.9 0.1 dynamic_slice.24
  13.0 37.1 %all-gather.3.cloned.1.call-done = bf16[2048,256]{0,1:T(8,128)(2,1)} async-done(((bf16[128,256]{0,1:T(8,128)(2,1)}), bf16[2048,256]{0,1:T(8,128)(2,1)}) %all-gather.3.cloned.1.call-update) | async-done | bytes 1048592 | tf_op jit(solution)/shard_map/all_gather | solution.py:93
  50.1 38.4 %all-gather.5.cloned.1.call-done = bf16[2048,256]{0,1:T(8,128)(2,1)} async-done(((bf16[128,256]{0,1:T(8,128)(2,1)}), bf16[2048,256]{0,1:T(8,128)(2,1)}) %all-gather.5.cloned.1.call-update) | async-done | bytes 1048592 | tf_op jit(solution)/shard_map/all_gather | solution.py:94
  88.5 23.3 %while.20 = (s32[]{:T(128)}, f32[2,7,128]{2,1,0:T(8,128)S(1)}, f32[2,7,128]{2,1,0:T(8,128)S(1)}, f32[2,7,128,128]{3,2,1,0:T(8,128)S(1)}, f32[32,512]{1,0:T(8,128...) while((s32[]{:T(128)}, f32[2,7,128]{2,1,0:T(8,128)S(1)}, ...), condition=%wide.region_3.4_spmd.clone, body=%wide.region_0.3_spmd.clone.sunk | while | flops 499344320 | bytes 16182928 | solution.py:107
  88.5 0.7 multiply_add_fusion.2
  89.3 0.1 dynamic_slice.33
  89.3 0.1 broadcast_compare_fusion.2
  89.5 1.1 constant_dynamic-slice_fusion.3
  90.6 0.2 convolution_bitcast_fusion.4
  90.8 0.2 convolution_bitcast_fusion.5
  91.1 0.8 fusion.47
  91.9 0.9 fusion.48
  92.8 1.5 %fusion.50 = f32[2,7,128,128]{3,2,1,0:T(8,128)S(1)} fusion(bf16[512,2,128,1]{0,2,3,1:T(8,128)(2,1)S(1)} %bitcast.80, f32[2,512,128,7]{2,1,3,0:T(8,128)S(1)} %get-tuple-element.372, f32[2,7,128]{2,1,0:T(8,128)S(1)} %select_maximum_fusion.2, pred[128,512]{0,1:T(8,128)(4,1)S(1)} %broadcast_compare_fusion.2, ...), kind=kOutput, calls=%fused_computation.8.clone.1 | convolution fusion | flops 240156672 | bytes 5847041 | tf_op jit(solution)/shard_map/while/body/eval_jaxpr/hgqk,khd->hgqd/dot_general | solution.py:78
  94.4 0.7 multiply_add_fusion.2
  95.1 0.1 dynamic_slice.33
  95.2 0.1 broadcast_compare_fusion.2
  95.3 1.1 constant_dynamic-slice_fusion.3
  96.4 0.2 convolution_bitcast_fusion.4
  96.6 0.2 convolution_bitcast_fusion.5
  96.9 0.8 fusion.47
  97.7 0.9 fusion.48
  98.6 1.5 %fusion.50 = f32[2,7,128,128]{3,2,1,0:T(8,128)S(1)} fusion(bf16[512,2,128,1]{0,2,3,1:T(8,128)(2,1)S(1)} %bitcast.80, f32[2,512,128,7]{2,1,3,0:T(8,128)S(1)} %get-tuple-element.372, f32[2,7,128]{2,1,0:T(8,128)S(1)} %select_maximum_fusion.2, pred[128,512]{0,1:T(8,128)(4,1)S(1)} %broadcast_compare_fusion.2, ...), kind=kOutput, calls=%fused_computation.8.clone.1 | convolution fusion | flops 240156672 | bytes 5847041 | tf_op jit(solution)/shard_map/while/body/eval_jaxpr/hgqk,khd->hgqd/dot_general | solution.py:78
  100.2 0.7 multiply_add_fusion.2
  100.9 0.1 dynamic_slice.33
  101.0 0.1 broadcast_compare_fusion.2
  101.1 1.1 constant_dynamic-slice_fusion.3
  102.2 0.2 convolution_bitcast_fusion.4
  102.4 0.2 convolution_bitcast_fusion.5
  102.7 0.8 fusion.47
  103.5 0.9 fusion.48
  104.4 1.5 %fusion.50 = f32[2,7,128,128]{3,2,1,0:T(8,128)S(1)} fusion(bf16[512,2,128,1]{0,2,3,1:T(8,128)(2,1)S(1)} %bitcast.80, f32[2,512,128,7]{2,1,3,0:T(8,128)S(1)} %get-tuple-element.372, f32[2,7,128]{2,1,0:T(8,128)S(1)} %select_maximum_fusion.2, pred[128,512]{0,1:T(8,128)(4,1)S(1)} %broadcast_compare_fusion.2, ...), kind=kOutput, calls=%fused_computation.8.clone.1 | convolution fusion | flops 240156672 | bytes 5847041 | tf_op jit(solution)/shard_map/while/body/eval_jaxpr/hgqk,khd->hgqd/dot_general | solution.py:78
  106.0 0.7 multiply_add_fusion.2
  106.8 0.1 broadcast_compare_fusion.2
  106.9 1.1 constant_dynamic-slice_fusion.3
  108.0 0.2 convolution_bitcast_fusion.4
  108.3 0.2 convolution_bitcast_fusion.5
  108.5 0.8 fusion.47
  109.3 0.9 fusion.48
  110.2 1.5 %fusion.50 = f32[2,7,128,128]{3,2,1,0:T(8,128)S(1)} fusion(bf16[512,2,128,1]{0,2,3,1:T(8,128)(2,1)S(1)} %bitcast.80, f32[2,512,128,7]{2,1,3,0:T(8,128)S(1)} %get-tuple-element.372, f32[2,7,128]{2,1,0:T(8,128)S(1)} %select_maximum_fusion.2, pred[128,512]{0,1:T(8,128)(4,1)S(1)} %broadcast_compare_fusion.2, ...), kind=kOutput, calls=%fused_computation.8.clone.1 | convolution fusion | flops 240156672 | bytes 5847041 | tf_op jit(solution)/shard_map/while/body/eval_jaxpr/hgqk,khd->hgqd/dot_general | solution.py:78
  111.8 0.3 copy.20
  112.1 0.1 divide_convert_fusion
  112.2 1.0 copy.21
  113.2 0.6 convert_element_type.25
  (37 shorter events, 0.6 us)
Async XLA Ops:
  7.2 42.9 %all-gather.3.cloned.1.call-start = ((), (), s32[]{:S(2)}) async-start(), calls=%async_computation | async-start | bytes 1114112 | tf_op jit(solution)/shard_map/all_gather | solution.py:93
  8.8 79.7 %all-gather.5.cloned.1.call-start = ((), (), s32[]{:S(2)}) async-start(), calls=%async_computation.1 | async-start | bytes 1114112 | tf_op jit(solution)/shard_map/all_gather | solution.py:94
Sparse Core Ops, SparseCore 0:
  10.7 39.3 all-gather.2
  52.3 36.2 all-gather.4
where the time goes:
time: 121 us
  waiting for transfers between devices  75.6 us (62%)
  between operations  14.1 us (12%)
  matrix products  11 us (9%)
  local copies, waits for them, and re-layouts  10.8 us (9%)
  other arithmetic  8.65 us (7%)
    all_gather x1, waiting for transfers between devices, local(): piece_values = lax.all_gather(value_rows, 'seq', axis=0, tiled=True)  38.4 us
    all_gather x1, waiting for transfers between devices, local(): piece_keys = lax.all_gather(key_rows, 'seq', axis=0, tiled=True)  37.1 us
    dot_general x4, matrix products, attend_block(): jnp.einsum('hgqk,khd->hgqd', weights.astype(jnp.bfloat16), block_values.r...  6.16 us
    unnamed x5, local copies, waits for them, and re-layouts  5.68 us
    dynamic_slice x4, local copies, waits for them, and re-layouts, inner(): block_values = lax.dynamic_slice_in_dim(piece_values, offset, width, 0)  4.29 us
    reduce_sum x4, other arithmetic, attend_block(): totals = totals * factor + jnp.sum(weights, axis=-1)  3.54 us
    dot_general x4, matrix products, attend_block(): jnp.einsum('qhgd,khd->hgqk', query_heads, block_keys.reshape(count, kv_he...  3.13 us
    add x4, other arithmetic, cache_sources(): return chosen * BLOCK + row_ids[None, :] % BLOCK  2.91 us
  transfers between devices with their start and end apart: 2, of which 2 were waited for; matrix products, arithmetic and copies ran while one was open for 3% of the time, Pallas kernels for 0%

commit v1 on v0

--- a/solution.py
+++ b/solution.py
@@ -91,7 +91,8 @@
     )
     initial = initial + (jnp.zeros((cache_local, 2 * kv_heads * HEAD_DIM), jnp.float32),)
     piece_keys = lax.all_gather(key_rows, "seq", axis=0, tiled=True)
-    piece_values = lax.all_gather(value_rows, "seq", axis=0, tiled=True)
+    outgoing = jnp.stack([value_rows] * lax.axis_size("seq"))
+    piece_values = jnp.concatenate(lax.all_to_all(outgoing, "seq", 0, 0), axis=0)
     count = piece_keys.shape[0]
     width = math.gcd(count, 512)
 

time: 121 us -> 99.5 us (0.82)
  waiting for transfers between devices: 75.6 us -> 38.9 us
  starting transfers between devices: 0.08 us -> 7.46 us
  other arithmetic: 8.65 us -> 12.4 us
  local copies, waits for them, and re-layouts: 10.8 us -> 14.5 us
    all_gather x1 -> x0, waiting for transfers between devices: 38.4 us -> none  [local(): piece_values = lax.all_gather(value_rows, 'seq', axis=0, tiled=True)]
    all_to_all x0 -> x1, waiting for transfers between devices: none -> 19.2 us  [local(): lax.all_to_all(outgoing, 'seq', 0, 0)]
    all_gather x1, waiting for transfers between devices: 37.1 us -> 19.7 us  [local(): piece_keys = lax.all_gather(key_rows, 'seq', axis=0, tiled=True)]
    all_to_all x0 -> x1, starting transfers between devices: none -> 7.41 us  [local(): lax.all_to_all(outgoing, 'seq', 0, 0)]
    dynamic_slice x0 -> x4, local copies, waits for them, and re-layouts: none -> 3.9 us  [inner(): block_keys = lax.dynamic_slice_in_dim(piece_keys, offset, width, 0)]
    dynamic_slice x4 -> x8, local copies, waits for them, and re-layouts: 4.29 us -> 0.68 us  [inner(): block_values = lax.dynamic_slice_in_dim(piece_values, offset, width, 0)]
    dynamic_slice x4, local copies, waits for them, and re-layouts: 0.3 us -> 3.04 us  [inner(): block_pos = lax.dynamic_slice_in_dim(positions, offset, width)]
    le x4, other arithmetic: 0.55 us -> 2.92 us  [attend_block(): visible = block_pos[None, None, None, :] <= query_pos[None, None, :, None]]
  transfers between devices with their start and end apart: 2 -> 2, of which waited for: 2 -> 2; matrix products, arithmetic and copies ran while one was open for 3% -> 5% of each run, Pallas kernels for 0% -> 0%
where the time goes in v1:
time: 99.5 us; the launch traced here: 98.9 us
  waiting for transfers between devices  38.9 us (39%)
  local copies, waits for them, and re-layouts  14.5 us (15%)
  between operations  14.1 us (14%)
  other arithmetic  12.4 us (12%)
  matrix products  11.1 us (11%)
  starting transfers between devices  7.46 us (7%)
    all_gather x1, waiting for transfers between devices, local(): piece_keys = lax.all_gather(key_rows, 'seq', axis=0, tiled=True)  19.7 us
    all_to_all x1, waiting for transfers between devices, local(): lax.all_to_all(outgoing, 'seq', 0, 0)  19.2 us
    all_to_all x1, starting transfers between devices, local(): lax.all_to_all(outgoing, 'seq', 0, 0)  7.41 us
    dot_general x4, matrix products, attend_block(): jnp.einsum('hgqk,khd->hgqd', weights.astype(jnp.bfloat16), block_values.r...  6.21 us
    unnamed x9, local copies, waits for them, and re-layouts  4.11 us
    dynamic_slice x4, local copies, waits for them, and re-layouts, inner(): block_keys = lax.dynamic_slice_in_dim(piece_keys, offset, width, 0)  3.9 us
    reduce_sum x4, other arithmetic, attend_block(): totals = totals * factor + jnp.sum(weights, axis=-1)  3.55 us
    dot_general x4, matrix products, attend_block(): jnp.einsum('qhgd,khd->hgqk', query_heads, block_keys.reshape(count, kv_he...  3.12 us
  transfers between devices with their start and end apart: 2, of which 2 were waited for; matrix products, arithmetic and copies ran while one was open for 5% of the time, Pallas kernels for 0%

profile of v1, /device:TPU:0, one launch (start us, length us, event | category | flops | bytes accessed | tf_op | source)
XLA Modules:
  0.0 98.9 jit_solution(11901568151330493140)
XLA Ops:
  7.2 1.0 %copy.44 = bf16[128,256]{0,1:T(8,128)(2,1)S(1)} copy(bf16[128,256]{1,0:T(8,128)(2,1)} %param.9) | data formatting | bytes 131072 | tf_op args[2]
  8.2 1.2 %stack.2 = bf16[16,128,256]{1,2,0:T(8,128)(2,1)} broadcast(bf16[128,256]{0,1:T(8,128)(2,1)S(1)} %copy.44), dimensions={1,2} | broadcast | bytes 1114112 | tf_op jit(solution)/shard_map/stack | solution.py:94
  9.4 7.4 %all-to-all-start = ((bf16[16,128,256]{1,2,0:T(8,128)(2,1)}), bf16[16,128,256]{1,2,0:T(8,128)(2,1)S(1)}, u32[]{:S(2)}, u32[]{:S(2)}) async-start(bf16[16,128,256]{1,2,0:T(8,128)(2,1)} %stack.2), calls=%async_computation | async-start | bytes 2097152 | tf_op jit(solution)/shard_map/all_to_all | solution.py:95
  16.9 1.6 %copy.42 = bf16[128,256]{0,1:T(8,128)(2,1)} copy(bf16[128,256]{1,0:T(8,128)(2,1)} %param.8) | data formatting | bytes 131072 | tf_op args[1]
  18.5 0.7 broadcast_multiply_fusion
  19.3 0.3 copy.43
  19.6 0.3 copy.46
  19.9 0.6 dynamic_slice.24
  20.5 0.6 and_select_fusion
  21.1 0.6 fusion.21
  21.6 19.2 %all-to-all-done = bf16[16,128,256]{1,2,0:T(8,128)(2,1)S(1)} async-done(((bf16[16,128,256]{1,2,0:T(8,128)(2,1)}), bf16[16,128,256]{1,2,0:T(8,128)(2,1)S(1)}, u32[]{:S(2)}, u32[]{:S(2)}) %all-to-all-start) | async-done | bytes 1048608 | tf_op jit(solution)/shard_map/all_to_all | solution.py:95
  40.9 0.5 copy.45
  41.4 19.7 %all-gather.2.cloned.1.call-done = bf16[2048,256]{0,1:T(8,128)(2,1)} async-done(((bf16[128,256]{0,1:T(8,128)(2,1)}), bf16[2048,256]{0,1:T(8,128)(2,1)}) %all-gather.2.cloned.1.call-update) | async-done | bytes 1048592 | tf_op jit(solution)/shard_map/all_gather | solution.py:93
  61.1 28.9 %while.20 = (s32[]{:T(128)}, f32[2,7,128]{2,1,0:T(8,128)S(1)}, f32[2,7,128]{2,1,0:T(8,128)S(1)}, f32[2,7,128,128]{3,2,1,0:T(8,128)S(1)}, f32[32,512]{1,0:T(8,128...) while((s32[]{:T(128)}, f32[2,7,128]{2,1,0:T(8,128)S(1)}, ...), condition=%wide.region_3.4_spmd.clone, body=%wide.region_0.3_spmd.clone.sunk | while | flops 499344320 | bytes 16707220 | solution.py:108
  61.1 0.8 multiply_add_fusion.2
  61.9 0.8 dynamic_slice.35
  62.6 0.7 broadcast_compare_fusion.2
  63.4 1.0 constant_dynamic-slice_fusion.4
  64.3 0.2 convolution_bitcast_fusion.5
  64.8 0.2 convolution_bitcast_fusion.4
  65.0 0.8 fusion.47
  65.8 0.9 fusion.48
  66.7 1.6 %fusion.50 = f32[2,7,128,128]{3,2,1,0:T(8,128)S(1)} fusion(bf16[512,2,128,1]{0,2,3,1:T(8,128)(2,1)S(1)} %bitcast.77, f32[2,512,128,7]{2,1,3,0:T(8,128)S(1)} %get-tuple-element.401, f32[2,7,128]{2,1,0:T(8,128)S(1)} %select_maximum_fusion.2, pred[128,512]{0,1:T(8,128)(4,1)S(1)} %broadcast_compare_fusion.2, ...), kind=kOutput, calls=%fused_computation.8.clone.1 | convolution fusion | flops 240156672 | bytes 5847041 | tf_op jit(solution)/shard_map/while/body/eval_jaxpr/hgqk,khd->hgqd/dot_general | solution.py:78
  68.3 0.8 multiply_add_fusion.2
  69.1 0.8 dynamic_slice.35
  69.9 0.7 broadcast_compare_fusion.2
  70.6 1.0 constant_dynamic-slice_fusion.4
  72.0 0.2 convolution_bitcast_fusion.4
  72.2 0.8 fusion.47
  73.0 0.9 fusion.48
  74.0 1.6 %fusion.50 = f32[2,7,128,128]{3,2,1,0:T(8,128)S(1)} fusion(bf16[512,2,128,1]{0,2,3,1:T(8,128)(2,1)S(1)} %bitcast.77, f32[2,512,128,7]{2,1,3,0:T(8,128)S(1)} %get-tuple-element.401, f32[2,7,128]{2,1,0:T(8,128)S(1)} %select_maximum_fusion.2, pred[128,512]{0,1:T(8,128)(4,1)S(1)} %broadcast_compare_fusion.2, ...), kind=kOutput, calls=%fused_computation.8.clone.1 | convolution fusion | flops 240156672 | bytes 5847041 | tf_op jit(solution)/shard_map/while/body/eval_jaxpr/hgqk,khd->hgqd/dot_general | solution.py:78
  75.5 0.8 multiply_add_fusion.2
  76.3 0.8 dynamic_slice.35
  77.1 0.7 broadcast_compare_fusion.2
  77.8 1.0 constant_dynamic-slice_fusion.4
  79.5 0.8 fusion.47
  80.3 0.9 fusion.48
  81.2 1.6 %fusion.50 = f32[2,7,128,128]{3,2,1,0:T(8,128)S(1)} fusion(bf16[512,2,128,1]{0,2,3,1:T(8,128)(2,1)S(1)} %bitcast.77, f32[2,512,128,7]{2,1,3,0:T(8,128)S(1)} %get-tuple-element.401, f32[2,7,128]{2,1,0:T(8,128)S(1)} %select_maximum_fusion.2, pred[128,512]{0,1:T(8,128)(4,1)S(1)} %broadcast_compare_fusion.2, ...), kind=kOutput, calls=%fused_computation.8.clone.1 | convolution fusion | flops 240156672 | bytes 5847041 | tf_op jit(solution)/shard_map/while/body/eval_jaxpr/hgqk,khd->hgqd/dot_general | solution.py:78
  82.8 0.8 multiply_add_fusion.2
  83.5 0.8 dynamic_slice.35
  84.3 0.7 broadcast_compare_fusion.2
  85.0 1.0 constant_dynamic-slice_fusion.4
  86.7 0.8 fusion.47
  87.5 0.9 fusion.48
  88.4 1.6 %fusion.50 = f32[2,7,128,128]{3,2,1,0:T(8,128)S(1)} fusion(bf16[512,2,128,1]{0,2,3,1:T(8,128)(2,1)S(1)} %bitcast.77, f32[2,512,128,7]{2,1,3,0:T(8,128)S(1)} %get-tuple-element.401, f32[2,7,128]{2,1,0:T(8,128)S(1)} %select_maximum_fusion.2, pred[128,512]{0,1:T(8,128)(4,1)S(1)} %broadcast_compare_fusion.2, ...), kind=kOutput, calls=%fused_computation.8.clone.1 | convolution fusion | flops 240156672 | bytes 5847041 | tf_op jit(solution)/shard_map/while/body/eval_jaxpr/hgqk,khd->hgqd/dot_general | solution.py:78
  90.0 0.3 copy.48
  90.4 1.0 %copy.49 = bf16[128,1792]{1,0:T(8,128)(2,1)} copy(bf16[128,1792]{0,1:T(8,128)(2,1)S(1)} %bitcast.80) | data formatting | bytes 917504
  91.4 0.6 convert_element_type.25
  (46 shorter events, 2.3 us)
Async XLA Ops:
  7.2 12.2 %copy-start = (bf16[128,1792]{1,0:T(8,128)(2,1)S(1)}, bf16[128,1792]{1,0:T(8,128)(2,1)}, u32[]{:S(2)}) copy-start(bf16[128,1792]{1,0:T(8,128)(2,1)} %param.7) | copy-start | bytes 1376260
  9.4 31.5 %all-to-all-start = ((bf16[16,128,256]{1,2,0:T(8,128)(2,1)}), bf16[16,128,256]{1,2,0:T(8,128)(2,1)S(1)}, u32[]{:S(2)}, u32[]{:S(2)}) async-start(bf16[16,128,256]{1,2,0:T(8,128)(2,1)} %stack.2), calls=%async_computation | async-start | bytes 2097152 | tf_op jit(solution)/shard_map/all_to_all | solution.py:95
  16.8 44.3 %all-gather.2.cloned.1.call-start = ((), (), s32[]{:S(2)}) async-start(), calls=%async_computation.1 | async-start | bytes 1114112 | tf_op jit(solution)/shard_map/all_gather | solution.py:93
  19.3 2.3 %copy-start.1 = (s32[2048]{0:T(1024)}, s32[2048]{0:T(1024)S(1)}, u32[]{:S(2)}) copy-start(s32[2048]{0:T(1024)S(1)} %add.107) | copy-start | bytes 24580
Sparse Core Ops, SparseCore 0:
  20.4 40.6 all-gather.1
